TPU v7x, 32 devices: a whole 2x2x4 slice. The times are simulated.
32 devices in a mesh: shard: 8 (over z, x), grp: 4 (over y, core).
Axes of the slice: x: 2, y: 2, z: 4, core: 2. Of those that a mesh axis runs over, the one named last changes fastest.
Arguments:
- table_t: bfloat16 [100, 622592], P(None, ('shard', 'grp')), may hold values from -6 to 6
- req_rows: int32 [1024, 128], P(('shard', 'grp')), may hold values from 0 to 19455
- count1: int32 [1024], P(('shard', 'grp')), may hold values from 1 to 128, as said below
- frontier_list: int32 [11, 32768], P(None, ('shard', 'grp')), may hold values from 0 to 4095, as said below
- req2_rows: int32 [1024, 128], P(('shard', 'grp')), may hold values from 0 to 1023
- count2: int32 [1024], P(('shard', 'grp')), may hold values from 1 to 128, as said below
- seed_list: int32 [16, 8192], P(None, ('shard', 'grp')), may hold values from 0 to 4095, as said below
- w1_self: bfloat16 [256, 100], replicated, may hold values from -0.625 to 0.625
- w1_neigh: bfloat16 [256, 100], replicated, may hold values from -1.25 to 1.25
- bias1: float32 [256], replicated, may hold values from -3 to 3
- w2_self: bfloat16 [47, 256], replicated, may hold values from -0.375 to 0.375
- w2_neigh: bfloat16 [47, 256], replicated, may hold values from -0.75 to 0.75
- bias2: float32 [47], replicated, may hold values from -3 to 3
Outputs:
- logits: float32 [47, 8192], P(None, ('shard', 'grp'))
Inputs may be any that keep to these rules, and one draw needn't show every extreme that they name: count1[r * 32 + o] counts the live slots of the block that device r asks of device o; in every draw some devices are asked for 128 rows by every device. `frontier_list`: every entry o * 128 + j names a live slot (j below count1 of that block) of the asking device. count2[r * 32 + o] counts the live slots of the block that device r asks of device o; in every draw some devices are asked for 128 rows by every device. `seed_list`: every entry o * 128 + j names a live slot (j below count2 of that block) of the asking device.
All inputs are finite; a program needn't handle non-finite values.
Results may differ from a plain program's by a relative error of at most 0.0029.
Values may be sent and summed in bfloat16 or wider, within the bound.
A program may use at most 64 MiB of HBM per device.

v0:
```python
import jax
import jax.numpy as jnp
from jax import lax
from jax.sharding import PartitionSpec as P


def mask_rows(received, counts, capacity):
    is_live = (jnp.arange(capacity, dtype=jnp.int32)[None, :] < counts[:, None]).reshape(-1)
    flat = received.reshape(-1, received.shape[-1])
    return jnp.where(is_live[:, None], flat, jnp.zeros((), flat.dtype))


def right_product(rows, weight):
    return lax.dot_general(
        rows, weight, (((1,), (1,)), ((), ())), preferred_element_type=jnp.float32
    )


def body(
    table_t,
    req_rows,
    count1,
    frontier_list,
    req2_rows,
    count2,
    seed_list,
    w1_self,
    w1_neigh,
    bias1,
    w2_self,
    w2_neigh,
    bias2,
):
    feat_width = table_t.shape[0]
    capacity = req_rows.shape[1]
    table_rows = table_t.T
    picked_rows = jnp.take(
        table_rows,
        lax.all_to_all(req_rows, ("shard", "grp"), split_axis=0, concat_axis=0, tiled=True),
        axis=0,
    )
    received = lax.all_to_all(
        picked_rows, ("shard", "grp"), split_axis=0, concat_axis=0, tiled=True
    )
    flat = mask_rows(received, count1, capacity)
    fanout_two = frontier_list.shape[0] - 1
    front_nodes = frontier_list.shape[1]
    picked = jnp.take(flat, frontier_list.reshape(-1), axis=0).reshape(
        fanout_two + 1, front_nodes, feat_width
    )
    summed = (jnp.sum(picked[1:].astype(jnp.float32), axis=0) / fanout_two).astype(jnp.bfloat16)
    preact = right_product(picked[0], w1_self) + right_product(summed, w1_neigh) + bias1[None, :]
    hidden_rows = jax.nn.relu(preact).astype(jnp.bfloat16)
    cap_two = req2_rows.shape[1]
    payload = jnp.concatenate(
        [right_product(hidden_rows, w2_self), right_product(hidden_rows, w2_neigh)], axis=1
    )
    chosen = jnp.take(
        payload,
        lax.all_to_all(req2_rows, ("shard", "grp"), split_axis=0, concat_axis=0, tiled=True),
        axis=0,
    )
    got_back = lax.all_to_all(chosen, ("shard", "grp"), split_axis=0, concat_axis=0, tiled=True)
    flat_two = mask_rows(got_back, count2, cap_two)
    fanout_one = seed_list.shape[0] - 1
    seed_nodes = seed_list.shape[1]
    picked_two = jnp.take(flat_two, seed_list.reshape(-1), axis=0).reshape(
        fanout_one + 1, seed_nodes, flat_two.shape[1]
    )
    classes = w2_self.shape[0]
    near = jnp.sum(picked_two[1:, :, classes:], axis=0) / fanout_one
    logits = (picked_two[0, :, :classes] + near).T + bias2[:, None]
    return logits


def solution(mesh):
    in_specs = (
        P(None, ("shard", "grp")),
        P(("shard", "grp"), None),
        P(("shard", "grp")),
        P(None, ("shard", "grp")),
        P(("shard", "grp"), None),
        P(("shard", "grp")),
        P(None, ("shard", "grp")),
        P(),
        P(),
        P(),
        P(),
        P(),
        P(),
    )
    out_specs = P(None, ("shard", "grp"))
    return jax.shard_map(body, mesh=mesh, in_specs=in_specs, out_specs=out_specs, check_vma=False)
```

profile of v0, /device:TPU:0, one launch (start us, length us, event | category | flops | bytes accessed | tf_op | source)
XLA Modules:
  0.0 196.0 jit_solution(5065027454529831224)
XLA Ops:
  0.0 0.0 copy-start
  0.0 7.3 %all-to-all-start.1 = ((s32[32,1,128]{2,1,0:T(1,128)}), s32[32,1,128]{2,1,0:T(1,128)S(1)}, u32[]{:S(2)}, u32[]{:S(2)}) async-start(s32[32,1,128]{2,1,0:T(1,128)} %bitcast.69), calls=%async_computation.1 | async-start | bytes 32768 | tf_op jit(solution)/shard_map/all_to_all | solution.py:39
  7.3 0.0 copy-start.1
  7.3 6.7 %copy.17 = bf16[100,19456]{0,1:T(8,128)(2,1)} copy(bf16[100,19456]{1,0:T(8,128)(2,1)} %param.13) | data formatting | bytes 7782400 | tf_op args[0]
  14.0 0.0 copy-done.1
  14.1 0.4 all-to-all-done.1
  14.4 5.5 %all-to-all-start = ((s32[32,1,128]{2,1,0:T(1,128)}), s32[32,1,128]{2,1,0:T(1,128)S(1)}, u32[]{:S(2)}, u32[]{:S(2)}) async-start(s32[32,1,128]{2,1,0:T(1,128)} %bitcast.1), calls=%async_computation | async-start | bytes 32768 | tf_op jit(solution)/shard_map/all_to_all | solution.py:60
  19.9 14.1 %gather_fusion = bf16[4096,100]{1,0:T(8,128)(2,1)S(1)} fusion(bf16[19456,100]{1,0:T(8,128)(2,1)} %bitcast.54, s32[4096]{0:T(1024)S(1)} %fusion.10), kind=kCustom, calls=%fused_computation | custom fusion | bytes 1654784 | tf_op jit(solution)/shard_map/jit(_take)/gather | solution.py:37
  34.1 0.7 copy.18
  34.7 0.0 copy-start.8
  34.8 1.0 broadcast_select_fusion.1
  35.8 0.0 all-to-all-done
  35.8 5.8 %all-to-all-start.2 = ((bf16[32,128,100]{1,2,0:T(8,128)(2,1)}), bf16[32,128,100]{1,2,0:T(8,128)(2,1)S(1)}, u32[]{:S(2)}, u32[]{:S(2)}) async-start(bf16[32,128,100]{1,2,0:T(8,128)(2,1)} %broadcast_select_fusion.1), calls=%async_computation.2 | async-start | bytes 1703936 | tf_op jit(solution)/shard_map/all_to_all | solution.py:42
  41.7 0.0 copy-done.8
  41.7 0.1 fusion.14
  41.8 21.8 %all-to-all-done.2 = bf16[32,128,100]{1,2,0:T(8,128)(2,1)S(1)} async-done(((bf16[32,128,100]{1,2,0:T(8,128)(2,1)}), bf16[32,128,100]{1,2,0:T(8,128)(2,1)S(1)}, u32[]{:S(2)}, u32[]{:S(2)}) %all-to-all-start.2) | async-done | bytes 819232 | tf_op jit(solution)/shard_map/all_to_all | solution.py:42
  63.6 0.7 copy.19
  64.3 2.1 %bitcast_select_fusion.1 = bf16[4096,100]{1,0:T(8,128)(2,1)S(1)} fusion(bf16[32,128,100]{2,1,0:T(8,128)(2,1)S(1)} %copy.19, pred[4096]{0:T(1024)(128)(4,1)S(1)} %fusion.14), kind=kLoop, calls=%fused_computation.11 | loop fusion | flops 409600 | bytes 1642496 | tf_op jit(solution)/shard_map/jit(_where)/select_n | solution.py:10
  66.5 40.1 %gather_fusion.1 = bf16[11264,100]{1,0:T(8,128)(2,1)} fusion(bf16[4096,100]{1,0:T(8,128)(2,1)S(1)} %bitcast_select_fusion.1, s32[11264]{0:T(1024)S(1)} %broadcast_clamp_fusion), kind=kCustom, calls=%fused_computation.1 | custom fusion | bytes 4550656 | tf_op jit(solution)/shard_map/jit(_take)/gather | solution.py:48
  106.6 7.6 %broadcast_select_fusion = bf16[11264,100]{1,0:T(8,128)(2,1)S(1)} fusion(bf16[11264,100]{1,0:T(8,128)(2,1)} %gather_fusion.1, pred[11264]{0:T(1024)(128)(4,1)S(1)} %compare_and_fusion), kind=kLoop, calls=%fused_computation.5 | loop fusion | flops 1126400 | bytes 4516864 | tf_op jit(solution)/shard_map/jit(_take)/select_n | solution.py:48
  114.2 0.2 slice.27
  114.4 0.0 copy-start.3
  114.5 0.0 copy-start.6
  114.5 0.6 convert_reduce_fusion
  115.0 0.0 copy-done
  115.0 0.0 copy-start.4
  115.1 0.0 copy-start.5
  115.1 0.3 fusion.3
  115.3 0.0 copy-done.3
  115.4 0.0 copy-done.6
  115.4 0.3 fusion.2
  115.7 0.1 copy-done.4
  115.8 0.2 fusion.16
  116.1 0.0 copy-done.5
  116.1 0.2 fusion.17
  116.4 0.2 copy.20
  116.6 10.8 %gather_fusion.2 = f32[4096,94]{1,0:T(8,128)S(1)} fusion(f32[1024,94]{1,0:T(8,128)S(1)} %copy.20, s32[4096]{0:T(1024)S(1)} %fusion.12), kind=kCustom, calls=%fused_computation.2 | custom fusion | bytes 3096576 | tf_op jit(solution)/shard_map/jit(_take)/gather | solution.py:58
  127.4 1.8 copy.21
  129.2 2.8 %broadcast_select_fusion.3 = f32[32,128,94]{1,2,0:T(8,128)} fusion(f32[32,128,94]{1,2,0:T(8,128)} %copy.21, pred[32,128]{1,0:T(8,128)(4,1)S(1)} %compare_and_fusion.2), kind=kLoop, calls=%fused_computation.14 | loop fusion | flops 385024 | bytes 3084288 | tf_op jit(solution)/shard_map/jit(_take)/select_n | solution.py:58
  131.9 0.0 copy-start.2
  131.9 0.0 copy-start.9
  131.9 3.6 %all-to-all-start.3 = ((f32[32,128,94]{1,2,0:T(8,128)}), f32[32,128,94]{1,2,0:T(8,128)S(1)}, u32[]{:S(2)}, u32[]{:S(2)}) async-start(f32[32,128,94]{1,2,0:T(8,128)} %broadcast_select_fusion.3), calls=%async_computation.3 | async-start | bytes 3145728 | tf_op jit(solution)/shard_map/all_to_all | solution.py:63
  135.6 0.0 copy-done.2
  135.6 0.0 copy-done.9
  135.6 0.1 fusion.13
  135.7 37.3 %all-to-all-done.3 = f32[32,128,94]{1,2,0:T(8,128)S(1)} async-done(((f32[32,128,94]{1,2,0:T(8,128)}), f32[32,128,94]{1,2,0:T(8,128)S(1)}, u32[]{:S(2)}, u32[]{:S(2)}) %all-to-all-start.3) | async-done | bytes 1540128 | tf_op jit(solution)/shard_map/all_to_all | solution.py:63
  173.0 1.9 copy.22
  174.9 3.6 %bitcast_select_fusion = f32[4096,94]{1,0:T(8,128)S(1)} fusion(f32[32,128,94]{2,1,0:T(8,128)} %copy.22, pred[4096]{0:T(1024)(128)(4,1)S(1)} %fusion.13), kind=kLoop, calls=%fused_computation.6 | loop fusion | flops 385024 | bytes 3084288 | tf_op jit(solution)/shard_map/jit(_where)/select_n | solution.py:10
  178.5 14.2 %gather_fusion.3 = f32[4096,94]{1,0:T(8,128)} fusion(f32[4096,94]{1,0:T(8,128)S(1)} %bitcast_select_fusion, s32[4096]{0:T(1024)S(1)} %broadcast_clamp_fusion.1), kind=kCustom, calls=%fused_computation.3 | custom fusion | bytes 3096576 | tf_op jit(solution)/shard_map/jit(_take)/gather | solution.py:67
  192.6 2.0 %copy.23 = f32[16,256,94]{1,2,0:T(8,128)S(1)} copy(f32[16,256,94]{2,1,0:T(8,128)} %bitcast.57) | data formatting | bytes 3080192 | tf_op jit(solution)/shard_map/jit(_take)/gather | solution.py:67
  194.6 0.0 copy-start.7
  194.6 0.1 broadcast_select_fusion.2
  194.8 0.1 slice_reduce_fusion
  194.9 0.4 copy-done.7
  195.3 0.7 fusion.8
  (14 shorter events, 0.3 us)
Async XLA Ops:
  0.0 115.0 %copy-start = (bf16[256,100]{0,1:T(8,128)(2,1)S(1)}, bf16[256,100]{0,1:T(8,128)(2,1)}, u32[]{:S(2)}) copy-start(bf16[256,100]{0,1:T(8,128)(2,1)} %param.20) | copy-start | bytes 153604
  0.0 14.4 %all-to-all-start.1 = ((s32[32,1,128]{2,1,0:T(1,128)}), s32[32,1,128]{2,1,0:T(1,128)S(1)}, u32[]{:S(2)}, u32[]{:S(2)}) async-start(s32[32,1,128]{2,1,0:T(1,128)} %bitcast.69), calls=%async_computation.1 | async-start | bytes 32768 | tf_op jit(solution)/shard_map/all_to_all | solution.py:39
  7.3 6.7 %copy-start.1 = (s32[11,1024]{1,0:T(8,128)S(1)}, s32[11,1024]{1,0:T(8,128)}, u32[]{:S(2)}) copy-start(s32[11,1024]{1,0:T(8,128)} %param.16) | copy-start | bytes 135172
  14.4 21.3 %all-to-all-start = ((s32[32,1,128]{2,1,0:T(1,128)}), s32[32,1,128]{2,1,0:T(1,128)S(1)}, u32[]{:S(2)}, u32[]{:S(2)}) async-start(s32[32,1,128]{2,1,0:T(1,128)} %bitcast.1), calls=%async_computation | async-start | bytes 32768 | tf_op jit(solution)/shard_map/all_to_all | solution.py:60
  34.7 7.0 %copy-start.8 = (s32[32]{0:T(128)S(1)}, s32[32]{0:T(128)}, u32[]{:S(2)}) copy-start(s32[32]{0:T(128)} %param.15) | copy-start | bytes 388
  35.8 27.8 %all-to-all-start.2 = ((bf16[32,128,100]{1,2,0:T(8,128)(2,1)}), bf16[32,128,100]{1,2,0:T(8,128)(2,1)S(1)}, u32[]{:S(2)}, u32[]{:S(2)}) async-start(bf16[32,128,100]{1,2,0:T(8,128)(2,1)} %broadcast_select_fusion.1), calls=%async_computation.2 | async-start | bytes 1703936 | tf_op jit(solution)/shard_map/all_to_all | solution.py:42
  114.4 0.9 copy-start.3
  114.5 0.9 copy-start.6
  115.0 0.7 copy-start.4
  115.1 1.0 copy-start.5
  131.9 3.6 %copy-start.2 = (s32[16,256]{1,0:T(8,128)S(1)}, s32[16,256]{1,0:T(8,128)}, u32[]{:S(2)}) copy-start(s32[16,256]{1,0:T(8,128)} %param.19) | copy-start | bytes 49156
  131.9 3.7 %copy-start.9 = (s32[32]{0:T(128)S(1)}, s32[32]{0:T(128)}, u32[]{:S(2)}) copy-start(s32[32]{0:T(128)} %param.18) | copy-start | bytes 388
  131.9 41.1 %all-to-all-start.3 = ((f32[32,128,94]{1,2,0:T(8,128)}), f32[32,128,94]{1,2,0:T(8,128)S(1)}, u32[]{:S(2)}, u32[]{:S(2)}) async-start(f32[32,128,94]{1,2,0:T(8,128)} %broadcast_select_fusion.3), calls=%async_computation.3 | async-start | bytes 3145728 | tf_op jit(solution)/shard_map/all_to_all | solution.py:63
  194.6 0.7 copy-start.7
where the time goes:
time: 197 us; the launch traced here: 196 us
  local copies, waits for them, and re-layouts  94 us (48%)
  waiting for transfers between devices  59.4 us (30%)
  starting transfers between devices  22.2 us (11%)
  other arithmetic  18.9 us (10%)
    gather x1, local copies, waits for them, and re-layouts, body(): jnp.take(flat, frontier_list.reshape(-1), axis=0)  40.1 us
    all_to_all x1, waiting for transfers between devices, body(): lax.all_to_all(chosen, ('shard', 'grp'), split_axis=0, concat_axis=0, til...  37.3 us
    all_to_all x1, waiting for transfers between devices, body(): lax.all_to_all(picked_rows, ('shard', 'grp'), split_axis=0, concat_axis=0...  21.8 us
    gather x2, local copies, waits for them, and re-layouts, body(): jnp.take(flat_two, seed_list.reshape(-1), axis=0)  16.2 us
    gather x2, local copies, waits for them, and re-layouts, body(): jnp.take(table_rows, lax.all_to_all(req_rows, ('shard', 'grp'), split_axi...  14.8 us
    gather x2, local copies, waits for them, and re-layouts, body(): jnp.take(payload, lax.all_to_all(req2_rows, ('shard', 'grp'), split_axis=...  12.6 us
    select_n x2, other arithmetic, body(): jnp.take(flat, frontier_list.reshape(-1), axis=0)  7.65 us
    unnamed x23, local copies, waits for them, and re-layouts  7.34 us
  transfers between devices with their start and end apart: 4, of which 3 were waited for; matrix products, arithmetic and copies ran while one was open for 12% of the time, Pallas kernels for 0%

commit v1 on v0

--- a/solution.py
+++ b/solution.py
@@ -1,7 +1,252 @@
+import functools
+
 import jax
 import jax.numpy as jnp
 from jax import lax
+from jax.experimental import pallas as pl
+from jax.experimental.pallas import tpu as pltpu
 from jax.sharding import PartitionSpec as P
+
+AXES = ("shard", "grp")
+LANES = 128
+MIB = 1024 * 1024
+MATRIX_LIMIT = 4 * MIB
+VMEM_ALL = pl.BlockSpec(memory_space=pltpu.VMEM)
+SMEM_ALL = pl.BlockSpec(memory_space=pltpu.SMEM)
+
+
+def params(mib=48, **extra):
+    return pltpu.CompilerParams(vmem_limit_bytes=mib * MIB, **extra)
+
+
+def cost(flops, moved):
+    return pl.CostEstimate(flops=int(flops), bytes_accessed=int(moved), transcendentals=0)
+
+
+def local_rows(values, base, span):
+    local = values - base
+    inside = jnp.logical_and(local >= 0, local < span)
+    return jnp.where(inside, local, -1).astype(jnp.float32)
+
+
+def iota_groups(span):
+    base = lax.broadcasted_iota(jnp.int32, (16, LANES), 0)
+    return [(base + 16 * g).astype(jnp.float32).astype(jnp.bfloat16) for g in range(span // 16)]
+
+
+def count_kernel(list_ref, own_ref, near_ref):
+    span = own_ref.shape[0]
+    local = local_rows(list_ref[...], pl.program_id(0) * span, span)
+    groups = iota_groups(span)
+    one, zero = jnp.ones((), jnp.bfloat16), jnp.zeros((), jnp.bfloat16)
+    for c in range(own_ref.shape[1] // LANES):
+        cols = slice(c * LANES, (c + 1) * LANES)
+        counts = [jnp.zeros((16, LANES), jnp.bfloat16) for _ in groups]
+        for k in range(list_ref.shape[0]):
+            row = jnp.broadcast_to(local[k : k + 1, cols], (16, LANES)).astype(jnp.bfloat16)
+            for g, ids in enumerate(groups):
+                hit = jnp.where(row == ids, one, zero)
+                if k == 0:
+                    own_ref[16 * g : 16 * g + 16, cols] = hit
+                else:
+                    counts[g] = counts[g] + hit
+        for g in range(len(groups)):
+            near_ref[16 * g : 16 * g + 16, cols] = counts[g]
+
+
+def count_matrices(picks, slots, cap):
+    entries, nodes = picks.shape
+    out = jax.ShapeDtypeStruct((slots, nodes), jnp.bfloat16)
+    return pl.pallas_call(
+        count_kernel,
+        grid=(slots // cap,),
+        in_specs=[pl.BlockSpec((entries, nodes), lambda o: (0, 0))],
+        out_specs=[pl.BlockSpec((cap, nodes), lambda o: (o, 0))] * 2,
+        out_shape=[out, out],
+        compiler_params=params(),
+        cost_estimate=cost(entries * slots * nodes * 4, slots * nodes * 4),
+    )(picks)
+
+
+def onehot_kernel(ids_ref, out_ref):
+    groups = iota_groups(LANES)
+    one, zero = jnp.ones((), jnp.bfloat16), jnp.zeros((), jnp.bfloat16)
+    wanted = ids_ref[pl.ds(pl.program_id(0), 1), :]
+    for c in range(out_ref.shape[1] // LANES):
+        cols = slice(c * LANES, (c + 1) * LANES)
+        for b in range(out_ref.shape[0] // LANES):
+            local = local_rows(wanted[:, cols], b * LANES, LANES)
+            row = jnp.broadcast_to(local, (16, LANES)).astype(jnp.bfloat16)
+            for g, ids in enumerate(groups):
+                at = b * LANES + 16 * g
+                out_ref[at : at + 16, cols] = jnp.where(row == ids, one, zero)
+
+
+def onehot_matrix(ids, nodes):
+    devices, cap = ids.shape
+    return pl.pallas_call(
+        onehot_kernel,
+        grid=(devices,),
+        in_specs=[pl.BlockSpec((devices, cap), lambda o: (0, 0))],
+        out_specs=pl.BlockSpec((nodes, cap), lambda o: (0, o)),
+        out_shape=jax.ShapeDtypeStruct((nodes, devices * cap), jnp.bfloat16),
+        compiler_params=params(),
+        cost_estimate=cost(nodes * devices * cap * 4, nodes * devices * cap * 2),
+    )(ids)
+
+
+def rows_kernel(table_ref, out_ref):
+    out_ref[...] = table_ref[...].astype(jnp.float32).T
+
+
+def table_rows(table_t):
+    width, rows = table_t.shape
+    step = next(s for s in (1024, 512, 256, 128) if rows % s == 0)
+    return pl.pallas_call(
+        rows_kernel,
+        grid=(rows // step,),
+        in_specs=[pl.BlockSpec((width, step), lambda i: (0, i))],
+        out_specs=pl.BlockSpec((step, width), lambda i: (i, 0)),
+        out_shape=jax.ShapeDtypeStruct((rows, width), jnp.float32),
+        compiler_params=params(),
+        cost_estimate=cost(rows * width * 64, rows * width * 6),
+    )(table_t)
+
+
+def gather_kernel(ids_ref, rows_ref, out_ref, block):
+    cap = ids_ref.shape[1]
+
+    def one_asker(asker, carry):
+        for j in range(cap):
+            block[j : j + 1, :] = rows_ref[pl.ds(ids_ref[asker, j], 1), :]
+        out_ref[asker] = block[...].T.astype(jnp.bfloat16)
+        return carry
+
+    lax.fori_loop(0, ids_ref.shape[0], one_asker, 0)
+
+
+def gather_columns(ids, rows):
+    devices, cap = ids.shape
+    width = rows.shape[1]
+    return pl.pallas_call(
+        gather_kernel,
+        in_specs=[SMEM_ALL, VMEM_ALL],
+        out_specs=VMEM_ALL,
+        out_shape=jax.ShapeDtypeStruct((devices, width, cap), jnp.bfloat16),
+        scratch_shapes=[pltpu.VMEM((cap, width), jnp.float32)],
+        compiler_params=params(),
+        cost_estimate=cost(devices * cap * width * 64, rows.size * 4),
+    )(ids, rows)
+
+
+def lay_side_by_side(counts_ref, blocks_ref, flat):
+    devices, width, cap = blocks_ref.shape
+    slot = lax.broadcasted_iota(jnp.int32, (width, cap), 1)
+
+    def one(o, carry):
+        block = blocks_ref[o].astype(jnp.float32)
+        live = jnp.where(slot < counts_ref[o], block, 0.0)
+        flat[:, pl.ds(pl.multiple_of(o * cap, cap), cap)] = live.astype(jnp.bfloat16)
+        return carry
+
+    lax.fori_loop(0, devices, one, 0)
+
+
+def dot32(a, b):
+    return jnp.dot(a, b, preferred_element_type=jnp.float32)
+
+
+def front_kernel(
+    fanout,
+    counts_ref,
+    got_ref,
+    own_ref,
+    near_ref,
+    onehot_ref,
+    w1s_ref,
+    w1n_ref,
+    bias_ref,
+    w2_ref,
+    out_ref,
+    flat,
+    payload,
+):
+    lay_side_by_side(counts_ref, got_ref, flat)
+    nodes = own_ref.shape[1]
+    wide = 256
+
+    def nodes_chunk(c, carry):
+        cols = pl.ds(pl.multiple_of(c * wide, wide), wide)
+        own = dot32(flat[...], own_ref[:, cols]).astype(jnp.bfloat16)
+        summed = (dot32(flat[...], near_ref[:, cols]) / fanout).astype(jnp.bfloat16)
+        preact = dot32(w1s_ref[...], own) + dot32(w1n_ref[...], summed) + bias_ref[...]
+        hidden = jnp.maximum(preact, 0.0).astype(jnp.bfloat16)
+        payload[:, cols] = dot32(w2_ref[...], hidden).astype(jnp.bfloat16)
+        return carry
+
+    lax.fori_loop(0, nodes // wide, nodes_chunk, 0)
+    cap = out_ref.shape[2]
+    pair = 2
+
+    def askers(p, carry):
+        cols = pl.ds(pl.multiple_of(p * pair * cap, pair * cap), pair * cap)
+        chosen = dot32(payload[...], onehot_ref[:, cols]).astype(jnp.bfloat16)
+        for h in range(pair):
+            out_ref[p * pair + h] = chosen[:, h * cap : (h + 1) * cap]
+        return carry
+
+    lax.fori_loop(0, out_ref.shape[0] // pair, askers, 0)
+
+
+def front_payload(counts, got, own, near, onehot, w1s, w1n, bias1, w2, fanout):
+    devices, width, cap = got.shape
+    slots, nodes = own.shape
+    return pl.pallas_call(
+        functools.partial(front_kernel, float(fanout)),
+        in_specs=[SMEM_ALL] + [VMEM_ALL] * 8,
+        out_specs=VMEM_ALL,
+        out_shape=jax.ShapeDtypeStruct((devices, w2.shape[0], cap), jnp.bfloat16),
+        scratch_shapes=[
+            pltpu.VMEM((width, slots), jnp.bfloat16),
+            pltpu.VMEM((w2.shape[0], nodes), jnp.bfloat16),
+        ],
+        compiler_params=params(),
+        cost_estimate=cost(slots * nodes * 600, slots * nodes * 6),
+    )(counts, got, own, near, onehot, w1s, w1n, bias1, w2)
+
+
+def seed_kernel(fanout, classes, counts_ref, got_ref, own_ref, near_ref, bias_ref, out_ref, flat):
+    lay_side_by_side(counts_ref, got_ref, flat)
+    half = flat.shape[0] // 2
+    mine = dot32(flat[:half], own_ref[...])
+    near = dot32(flat[half:], near_ref[...]) / fanout
+    out_ref[...] = (mine + near)[:classes] + bias_ref[...]
+
+
+def seed_logits(counts, got, own, near, bias2, fanout):
+    classes = bias2.shape[0]
+    devices, width, cap = got.shape
+    slots, seeds = own.shape
+    return pl.pallas_call(
+        functools.partial(seed_kernel, float(fanout), classes),
+        in_specs=[SMEM_ALL] + [VMEM_ALL] * 4,
+        out_specs=VMEM_ALL,
+        out_shape=jax.ShapeDtypeStruct((classes, seeds), jnp.float32),
+        scratch_shapes=[pltpu.VMEM((width, slots), jnp.bfloat16)],
+        compiler_params=params(),
+        cost_estimate=cost(slots * seeds * 400, slots * seeds * 4),
+    )(counts, got, own, near, bias2)
+
+
+def exchange(blocks):
+    return lax.all_to_all(blocks, AXES, split_axis=0, concat_axis=0, tiled=True)
+
+
+def stacked_w2(w2_self, w2_neigh):
+    classes = w2_self.shape[0]
+    half = -(-classes // 16) * 16
+    pad = ((0, half - classes), (0, 0))
+    return jnp.concatenate([jnp.pad(w2_self, pad), jnp.pad(w2_neigh, pad)], axis=0)
 
 
 def mask_rows(received, counts, capacity):
@@ -16,7 +261,7 @@
     )
 
 
-def body(
+def take_body(
     table_t,
     req_rows,
     count1,
@@ -36,11 +281,11 @@
     table_rows = table_t.T
     picked_rows = jnp.take(
         table_rows,
-        lax.all_to_all(req_rows, ("shard", "grp"), split_axis=0, concat_axis=0, tiled=True),
+        lax.all_to_all(req_rows, AXES, split_axis=0, concat_axis=0, tiled=True),
         axis=0,
     )
     received = lax.all_to_all(
-        picked_rows, ("shard", "grp"), split_axis=0, concat_axis=0, tiled=True
+        picked_rows, AXES, split_axis=0, concat_axis=0, tiled=True
     )
     flat = mask_rows(received, count1, capacity)
     fanout_two = frontier_list.shape[0] - 1
@@ -57,10 +302,10 @@
     )
     chosen = jnp.take(
         payload,
-        lax.all_to_all(req2_rows, ("shard", "grp"), split_axis=0, concat_axis=0, tiled=True),
+        lax.all_to_all(req2_rows, AXES, split_axis=0, concat_axis=0, tiled=True),
         axis=0,
     )
-    got_back = lax.all_to_all(chosen, ("shard", "grp"), split_axis=0, concat_axis=0, tiled=True)
+    got_back = lax.all_to_all(chosen, AXES, split_axis=0, concat_axis=0, tiled=True)
     flat_two = mask_rows(got_back, count2, cap_two)
     fanout_one = seed_list.shape[0] - 1
     seed_nodes = seed_list.shape[1]
@@ -73,21 +318,84 @@
     return logits
 
 
+def body(
+    table_t,
+    req_rows,
+    count1,
+    frontier_list,
+    req2_rows,
+    count2,
+    seed_list,
+    w1_self,
+    w1_neigh,
+    bias1,
+    w2_self,
+    w2_neigh,
+    bias2,
+):
+    devices, cap = req_rows.shape
+    cap_two = req2_rows.shape[1]
+    nodes = frontier_list.shape[1]
+    if devices * max(cap, cap_two) * nodes > MATRIX_LIMIT:
+        return take_body(
+            table_t,
+            req_rows,
+            count1,
+            frontier_list,
+            req2_rows,
+            count2,
+            seed_list,
+            w1_self,
+            w1_neigh,
+            bias1,
+            w2_self,
+            w2_neigh,
+            bias2,
+        )
+    asked = exchange(jnp.concatenate([req_rows, req2_rows], axis=1))
+    rows = table_rows(table_t)
+    picked = gather_columns(asked[:, :cap], rows)
+    got = exchange(picked)
+    fan_two = frontier_list.shape[0] - 1
+    fan_one = seed_list.shape[0] - 1
+    frontier_list, seed_list, asked_two, _ = lax.optimization_barrier(
+        (frontier_list, seed_list, asked[:, cap:], picked)
+    )
+    own, near = count_matrices(frontier_list, devices * cap, cap)
+    onehot = onehot_matrix(asked_two, nodes)
+    seed_own, seed_near = count_matrices(seed_list, devices * cap_two, cap_two)
+    payload = front_payload(
+        count1,
+        got,
+        own,
+        near,
+        onehot,
+        w1_self,
+        w1_neigh,
+        bias1[:, None],
+        stacked_w2(w2_self, w2_neigh),
+        fan_two,
+    )
+    got_two = exchange(payload)
+    return seed_logits(count2, got_two, seed_own, seed_near, bias2[:, None], fan_one)
+
+
 def solution(mesh):
     in_specs = (
-        P(None, ("shard", "grp")),
-        P(("shard", "grp"), None),
-        P(("shard", "grp")),
-        P(None, ("shard", "grp")),
-        P(("shard", "grp"), None),
-        P(("shard", "grp")),
-        P(None, ("shard", "grp")),
-        P(),
-        P(),
-        P(),
-        P(),
-        P(),
-        P(),
-    )
-    out_specs = P(None, ("shard", "grp"))
-    return jax.shard_map(body, mesh=mesh, in_specs=in_specs, out_specs=out_specs, check_vma=False)
+        P(None, AXES),
+        P(AXES, None),
+        P(AXES),
+        P(None, AXES),
+        P(AXES, None),
+        P(AXES),
+        P(None, AXES),
+        P(),
+        P(),
+        P(),
+        P(),
+        P(),
+        P(),
+    )
+    return jax.shard_map(
+        body, mesh=mesh, in_specs=in_specs, out_specs=P(None, AXES), check_vma=False
+    )

time: 197 us -> 118 us (0.60)
  local copies, waits for them, and re-layouts: 94 us -> 6.23 us
  Pallas kernels: 0 us -> 76.6 us
  waiting for transfers between devices: 59.4 us -> 14.7 us
  other arithmetic: 18.9 us -> 0.75 us
  starting transfers between devices: 22.2 us -> 19 us
    gather x7 -> x0, local copies, waits for them, and re-layouts: 83.6 us -> none  [the longest x1 40.1 us: body(): jnp.take(flat, frontier_list.reshape(-1), axis=0)]
    pallas_call x0 -> x7, Pallas kernels: none -> 76.6 us  [the longest x2 22.7 us: count_matrices(): pl.pallas_call(count_kernel, grid=(slots // cap,), in_specs=[pl.BlockSpec...]
    all_to_all x4 -> x3, waiting for transfers between devices: 59.4 us -> 14.7 us  [exchange(): return lax.all_to_all(blocks, AXES, split_axis=0, concat_axis=0, tiled=True)]
    select_n x8 -> x0, other arithmetic: 17.3 us -> none  [the longest x2 7.65 us: body(): jnp.take(flat, frontier_list.reshape(-1), axis=0)]
    all_to_all x4 -> x3, starting transfers between devices: 22.2 us -> 19 us  [exchange(): return lax.all_to_all(blocks, AXES, split_axis=0, concat_axis=0, tiled=True)]
    unnamed x23 -> x29, local copies, waits for them, and re-layouts: 7.34 us -> 5.35 us
  transfers between devices with their start and end apart: 4 -> 3, of which waited for: 3 -> 1; matrix products, arithmetic and copies ran while one was open for 12% -> 0% of each run, Pallas kernels for 0% -> 38%
where the time goes in v1:
time: 118 us
  Pallas kernels  76.6 us (65%)
  starting transfers between devices  19 us (16%)
  waiting for transfers between devices  14.7 us (12%)
  local copies, waits for them, and re-layouts  6.23 us (5%)
    pallas_call x2, Pallas kernels, count_matrices(): pl.pallas_call(count_kernel, grid=(slots // cap,), in_specs=[pl.BlockSpec...  22.7 us
    all_to_all x3, starting transfers between devices, exchange(): return lax.all_to_all(blocks, AXES, split_axis=0, concat_axis=0, tiled=True)  19 us
    pallas_call x1, Pallas kernels, front_payload(): pl.pallas_call(functools.partial(front_kernel, float(fanout)), in_specs=[...  18.1 us
    all_to_all x3, waiting for transfers between devices, exchange(): return lax.all_to_all(blocks, AXES, split_axis=0, concat_axis=0, tiled=True)  14.7 us
    pallas_call x1, Pallas kernels, onehot_matrix(): pl.pallas_call(onehot_kernel, grid=(devices,), in_specs=[pl.BlockSpec((de...  12.9 us
    pallas_call x1, Pallas kernels, gather_columns(): pl.pallas_call(gather_kernel, in_specs=[SMEM_ALL, VMEM_ALL], out_specs=VM...  11.1 us
    pallas_call x1, Pallas kernels, table_rows(): pl.pallas_call(rows_kernel, grid=(rows // step,), in_specs=[pl.BlockSpec(...  9.55 us
    unnamed x29, local copies, waits for them, and re-layouts  5.35 us
  transfers between devices with their start and end apart: 3, of which 1 were waited for; matrix products, arithmetic and copies ran while one was open for 0% of the time, Pallas kernels for 38%

profile of v1, /device:TPU:0, one launch (start us, length us, event | category | flops | bytes accessed | tf_op | source)
XLA Modules:
  0.0 117.5 jit_solution(2708018212434251528)
XLA Ops:
  0.0 0.7 pad_add_fusion
  0.7 0.6 all_to_all.14
  1.4 7.3 %all-to-all-start = ((s32[32,1,256]{2,1,0:T(1,128)}), s32[32,1,256]{2,1,0:T(1,128)S(1)}, u32[]{:S(2)}, u32[]{:S(2)}) async-start(s32[32,1,256]{2,1,0:T(1,128)} %all_to_all.14), calls=%async_computation | async-start | bytes 65536 | tf_op jit(solution)/shard_map/all_to_all | solution.py:242
  8.7 0.0 copy-start
  8.7 2.1 %copy-done = bf16[100,19456]{1,0:T(8,128)(2,1)S(1)} copy-done((bf16[100,19456]{1,0:T(8,128)(2,1)S(1)}, bf16[100,19456]{1,0:T(8,128)(2,1)}, u32[]{:S(2)}) %copy-start) | copy-done | bytes 3891224
  10.9 9.6 %shard_map.127.rows_ref = f32[19456,100]{1,0:T(8,128)} custom-call(bf16[100,19456]{1,0:T(8,128)(2,1)S(1)} %copy-done), custom_call_target="tpu_custom_call" | custom-call | flops 124518400 | bytes 11673600 | tf_op jit(solution)/shard_map/pallas_call | solution.py:105
  20.4 0.0 copy-start.11
  20.4 0.0 copy-start.7
  20.4 0.0 copy-start.8
  20.4 0.0 copy-start.9
  20.4 0.0 copy-start.10
  20.4 0.0 all-to-all-done
  20.5 0.0 copy-start.5
  20.5 0.0 copy-start.3
  20.5 11.1 %shard_map.128 = bf16[32,100,128]{2,1,0:T(8,128)(2,1)} custom-call(s32[32,128]{1,0:T(8,128)S(1)} %get-tuple-element.20.ids_ref, f32[19456,100]{1,0:T(8,128)} %shard_map.127.rows_ref), custom_call_target="tpu_custom_call" | custom-call | flops 26214400 | bytes 7782400 | tf_op jit(solution)/shard_map/pallas_call | solution.py:131
  31.5 5.8 %all-to-all-start.1 = ((bf16[32,100,128]{2,1,0:T(8,128)(2,1)}), bf16[32,100,128]{2,1,0:T(8,128)(2,1)S(1)}, u32[]{:S(2)}, u32[]{:S(2)}) async-start(bf16[32,100,128]{2,1,0:T(8,128)(2,1)} %shard_map.128), calls=%async_computation.1 | async-start | bytes 1703936 | tf_op jit(solution)/shard_map/all_to_all | solution.py:242
  37.4 0.0 copy-done.11
  37.4 0.1 copy.23.bias_ref
  37.5 0.0 copy-done.7
  37.5 0.1 copy.21.w1s_ref
  37.7 0.0 copy-done.8
  37.7 0.1 copy.22.w1n_ref
  37.8 0.0 copy-done.9
  37.8 0.0 copy-done.10
  37.8 12.9 %shard_map.130.onehot_ref = bf16[1024,4096]{1,0:T(8,128)(2,1)} custom-call(s32[32,128]{1,0:T(8,128)S(1)} %get-tuple-element.15.ids_ref), custom_call_target="tpu_custom_call" | custom-call | flops 16777216 | bytes 8388608 | tf_op jit(solution)/shard_map/pallas_call | solution.py:87
  50.7 0.0 copy-done.5
  50.7 18.3 %shard_map.129 = (bf16[4096,1024]{1,0:T(8,128)(2,1)}, bf16[4096,1024]{1,0:T(8,128)(2,1)}) custom-call(s32[11,1024]{1,0:T(8,128)S(1)} %copy-done.5), custom_call_target="tpu_custom_call" | custom-call | flops 184549376 | bytes 16777216 | tf_op jit(solution)/shard_map/pallas_call | solution.py:60
  69.0 0.0 all-to-all-done.1.got_ref
  69.0 0.0 copy-done.3
  69.0 0.0 copy-start.12
  69.0 0.0 copy-start.6
  69.1 0.0 copy-start.4
  69.1 18.1 %shard_map.131 = bf16[32,96,128]{2,1,0:T(8,128)(2,1)} custom-call(s32[32]{0:T(128)S(1)} %copy-done.3, bf16[32,100,128]{2,1,0:T(8,128)(2,1)S(1)} %all-to-all-done.1.got_ref, bf16[4096,1024]{1,0:T(8,128)(2,1)} %get-tuple-element.13.own_ref, bf16[4096,1024]{1,0:T(8,128)(2,1)} %get-tuple-element.14.near_ref, bf16[1024,4096]{1,0:T(8,128)(2,1)} %shard_map.130.onehot_ref, ...), custom_call_target="tpu_custom_call" | custom-call | flops 2516582400 | bytes 25165824 | tf_op jit(solution)/shard_map/pallas_call | solution.py:204
  87.2 5.8 %all-to-all-start.2 = ((bf16[32,96,128]{2,1,0:T(8,128)(2,1)}), bf16[32,96,128]{2,1,0:T(8,128)(2,1)S(1)}, u32[]{:S(2)}, u32[]{:S(2)}) async-start(bf16[32,96,128]{2,1,0:T(8,128)(2,1)} %shard_map.131), calls=%async_computation.2 | async-start | bytes 1572864 | tf_op jit(solution)/shard_map/all_to_all | solution.py:242
  93.0 0.0 copy-done.12
  93.0 0.1 copy.24.bias_ref
  93.2 0.0 copy-done.6
  93.2 4.4 %shard_map.132 = (bf16[4096,256]{1,0:T(8,128)(2,1)S(1)}, bf16[4096,256]{1,0:T(8,128)(2,1)S(1)}) custom-call(s32[16,256]{1,0:T(8,128)S(1)} %copy-done.6), custom_call_target="tpu_custom_call" | custom-call | flops 67108864 | bytes 4194304 | tf_op jit(solution)/shard_map/pallas_call | solution.py:60
  97.6 0.0 copy-start.1
  97.6 1.3 %copy-done.1 = bf16[4096,256]{1,0:T(8,128)(2,1)} copy-done((bf16[4096,256]{1,0:T(8,128)(2,1)}, bf16[4096,256]{1,0:T(8,128)(2,1)S(1)}, u32[]{:S(2)}) %copy-start.1) | copy-done | bytes 2097176
  98.9 14.7 %all-to-all-done.2.got_ref = bf16[32,96,128]{2,1,0:T(8,128)(2,1)S(1)} async-done(((bf16[32,96,128]{2,1,0:T(8,128)(2,1)}), bf16[32,96,128]{2,1,0:T(8,128)(2,1)S(1)}, u32[]{:S(2)}, u32[]{:S(2)}) %all-to-all-start.2) | async-done | bytes 786464 | tf_op jit(solution)/shard_map/all_to_all | solution.py:242
  113.6 0.0 copy-done.4
  113.6 0.0 copy-start.2
  113.6 1.6 %copy-done.2 = bf16[4096,256]{1,0:T(8,128)(2,1)S(1)} copy-done((bf16[4096,256]{1,0:T(8,128)(2,1)S(1)}, bf16[4096,256]{1,0:T(8,128)(2,1)}, u32[]{:S(2)}) %copy-start.2) | copy-done | bytes 2097176
  115.2 2.3 %shard_map.133 = f32[47,256]{1,0:T(8,128)} custom-call(s32[32]{0:T(128)S(1)} %copy-done.4, bf16[32,96,128]{2,1,0:T(8,128)(2,1)S(1)} %all-to-all-done.2.got_ref, bf16[4096,256]{1,0:T(8,128)(2,1)S(1)} %get-tuple-element.17.own_ref, bf16[4096,256]{1,0:T(8,128)(2,1)S(1)} %copy-done.2, f32[47,1]{1,0:T(8,128)S(1)} %copy.24.bias_ref), custom_call_target="tpu_custom_call" | custom-call | flops 419430400 | bytes 4194304 | tf_op jit(solution)/shard_map/pallas_call | solution.py:230
  (3 shorter events, 0.0 us)
Async XLA Ops:
  1.4 19.1 %all-to-all-start = ((s32[32,1,256]{2,1,0:T(1,128)}), s32[32,1,256]{2,1,0:T(1,128)S(1)}, u32[]{:S(2)}, u32[]{:S(2)}) async-start(s32[32,1,256]{2,1,0:T(1,128)} %all_to_all.14), calls=%async_computation | async-start | bytes 65536 | tf_op jit(solution)/shard_map/all_to_all | solution.py:242
  8.7 2.1 %copy-start = (bf16[100,19456]{1,0:T(8,128)(2,1)S(1)}, bf16[100,19456]{1,0:T(8,128)(2,1)}, u32[]{:S(2)}) copy-start(bf16[100,19456]{1,0:T(8,128)(2,1)} %table_ref.1) | copy-start | bytes 11673604
  20.4 17.0 %copy-start.11 = (f32[256]{0:T(256)S(1)}, f32[256]{0:T(256)}, u32[]{:S(2)}) copy-start(f32[256]{0:T(256)} %param.22) | copy-start | bytes 3076
  20.4 17.1 %copy-start.7 = (bf16[256,100]{0,1:T(8,128)(2,1)S(1)}, bf16[256,100]{0,1:T(8,128)(2,1)}, u32[]{:S(2)}) copy-start(bf16[256,100]{0,1:T(8,128)(2,1)} %param.20) | copy-start | bytes 153604
  20.4 17.3 %copy-start.8 = (bf16[256,100]{0,1:T(8,128)(2,1)S(1)}, bf16[256,100]{0,1:T(8,128)(2,1)}, u32[]{:S(2)}) copy-start(bf16[256,100]{0,1:T(8,128)(2,1)} %param.21) | copy-start | bytes 153604
  20.4 17.4 %copy-start.9 = (bf16[47,256]{1,0:T(8,128)(2,1)S(1)}, bf16[47,256]{1,0:T(8,128)(2,1)}, u32[]{:S(2)}) copy-start(bf16[47,256]{1,0:T(8,128)(2,1)} %param.24) | copy-start | bytes 72196
  20.4 17.4 %copy-start.10 = (bf16[47,256]{1,0:T(8,128)(2,1)S(1)}, bf16[47,256]{1,0:T(8,128)(2,1)}, u32[]{:S(2)}) copy-start(bf16[47,256]{1,0:T(8,128)(2,1)} %param.23) | copy-start | bytes 72196
  20.5 30.2 %copy-start.5 = (s32[11,1024]{1,0:T(8,128)S(1)}, s32[11,1024]{1,0:T(8,128)}, u32[]{:S(2)}) copy-start(s32[11,1024]{1,0:T(8,128)} %list_ref) | copy-start | bytes 135172
  20.5 48.6 %copy-start.3 = (s32[32]{0:T(128)S(1)}, s32[32]{0:T(128)}, u32[]{:S(2)}) copy-start(s32[32]{0:T(128)} %counts_ref.2) | copy-start | bytes 388
  31.5 37.5 %all-to-all-start.1 = ((bf16[32,100,128]{2,1,0:T(8,128)(2,1)}), bf16[32,100,128]{2,1,0:T(8,128)(2,1)S(1)}, u32[]{:S(2)}, u32[]{:S(2)}) async-start(bf16[32,100,128]{2,1,0:T(8,128)(2,1)} %shard_map.128), calls=%async_computation.1 | async-start | bytes 1703936 | tf_op jit(solution)/shard_map/all_to_all | solution.py:242
  69.0 24.0 %copy-start.12 = (f32[47]{0:T(128)S(1)}, f32[47]{0:T(128)}, u32[]{:S(2)}) copy-start(f32[47]{0:T(128)} %param.25) | copy-start | bytes 568
  69.0 24.1 %copy-start.6 = (s32[16,256]{1,0:T(8,128)S(1)}, s32[16,256]{1,0:T(8,128)}, u32[]{:S(2)}) copy-start(s32[16,256]{1,0:T(8,128)} %list_ref.1) | copy-start | bytes 49156
  69.1 44.6 %copy-start.4 = (s32[32]{0:T(128)S(1)}, s32[32]{0:T(128)}, u32[]{:S(2)}) copy-start(s32[32]{0:T(128)} %counts_ref.3) | copy-start | bytes 388
  87.2 26.4 %all-to-all-start.2 = ((bf16[32,96,128]{2,1,0:T(8,128)(2,1)}), bf16[32,96,128]{2,1,0:T(8,128)(2,1)S(1)}, u32[]{:S(2)}, u32[]{:S(2)}) async-start(bf16[32,96,128]{2,1,0:T(8,128)(2,1)} %shard_map.131), calls=%async_computation.2 | async-start | bytes 1572864 | tf_op jit(solution)/shard_map/all_to_all | solution.py:242
  97.6 1.3 %copy-start.1 = (bf16[4096,256]{1,0:T(8,128)(2,1)}, bf16[4096,256]{1,0:T(8,128)(2,1)S(1)}, u32[]{:S(2)}) copy-start(bf16[4096,256]{1,0:T(8,128)(2,1)S(1)} %get-tuple-element.18.near_ref) | copy-start | bytes 6291460
  113.6 1.6 %copy-start.2 = (bf16[4096,256]{1,0:T(8,128)(2,1)S(1)}, bf16[4096,256]{1,0:T(8,128)(2,1)}, u32[]{:S(2)}) copy-start(bf16[4096,256]{1,0:T(8,128)(2,1)} %copy-done.1) | copy-start | bytes 6291460

commit v2 on v0

--- a/solution.py
+++ b/solution.py
@@ -1,7 +1,256 @@
+import functools
+
 import jax
 import jax.numpy as jnp
 from jax import lax
+from jax.experimental import pallas as pl
+from jax.experimental.pallas import tpu as pltpu
 from jax.sharding import PartitionSpec as P
+
+AXES = ("shard", "grp")
+LANES = 128
+MIB = 1024 * 1024
+MATRIX_LIMIT = 4 * MIB
+VMEM_ALL = pl.BlockSpec(memory_space=pltpu.VMEM)
+SMEM_ALL = pl.BlockSpec(memory_space=pltpu.SMEM)
+
+
+def tall(row, span):
+    few = jnp.broadcast_to(row, (16, row.shape[1])).astype(jnp.bfloat16)
+    return jnp.concatenate([few] * (span // 16), axis=0)
+
+
+def local_rows(values, base, span):
+    local = values - base
+    inside = jnp.logical_and(local >= 0, local < span)
+    return jnp.where(inside, local, -1).astype(jnp.float32)
+
+
+def hits(row, span):
+    ids = lax.broadcasted_iota(jnp.int32, (span, row.shape[1]), 0)
+    ids = ids.astype(jnp.float32).astype(jnp.bfloat16)
+    return jnp.where(tall(row, span) == ids, jnp.ones((), jnp.bfloat16), jnp.zeros((), jnp.bfloat16))
+
+
+def tile(i, size=LANES):
+    return pl.ds(pl.multiple_of(i * size, size), size)
+
+
+def count_slots(list_ref, own_ref, near_ref, cap):
+    entries, nodes = list_ref.shape
+    across = nodes // LANES
+
+    def one(i, carry):
+        owner, cols = i // across, tile(i % across)
+        at = tile(owner, cap)
+        local = local_rows(list_ref[:, cols], owner * cap, cap)
+        own_ref[at, cols] = hits(local[0:1], cap)
+        total = hits(local[1:2], cap)
+        for k in range(2, entries):
+            total = total + hits(local[k : k + 1], cap)
+        near_ref[at, cols] = total
+        return carry
+
+    lax.fori_loop(0, own_ref.shape[0] // cap * across, one, 0)
+
+
+def onehot_slots(ids_ref, out_ref):
+    nodes = out_ref.shape[0]
+    devices, _, cap = ids_ref.shape
+
+    def one(asker, carry):
+        wanted = ids_ref[asker]
+        for b in range(nodes // LANES):
+            out_ref[b * LANES : (b + 1) * LANES, tile(asker, cap)] = hits(
+                local_rows(wanted, b * LANES, LANES), LANES
+            )
+        return carry
+
+    lax.fori_loop(0, devices, one, 0)
+
+
+def lay_side_by_side(counts_ref, blocks_ref, flat):
+    devices, width, cap = blocks_ref.shape
+    slot = lax.broadcasted_iota(jnp.int32, (width, cap), 1)
+
+    def one(o, carry):
+        live = jnp.where(slot < counts_ref[o], blocks_ref[o].astype(jnp.float32), 0.0)
+        flat[:, tile(o, cap)] = live.astype(jnp.bfloat16)
+        return carry
+
+    lax.fori_loop(0, devices, one, 0)
+
+
+def dot32(a, b):
+    return jnp.dot(a, b, preferred_element_type=jnp.float32)
+
+
+def whole_kernel(
+    grp,
+    table_ref,
+    req_ref,
+    req2_ref,
+    count1_ref,
+    count2_ref,
+    front_ref,
+    seed_ref,
+    w1s_ref,
+    w1n_ref,
+    bias1_ref,
+    w2_ref,
+    bias2_ref,
+    out_ref,
+    asked,
+    asked2,
+    ids,
+    rows,
+    block,
+    send,
+    got,
+    own,
+    near,
+    onehot,
+    seed_own,
+    seed_near,
+    flat,
+    payload,
+    send2,
+    got2,
+    flat2,
+    local_sem,
+    sems,
+):
+    devices, _, cap = req_ref.shape
+    me = lax.axis_index(AXES[0]) * grp + lax.axis_index(AXES[1])
+
+    def partner(t):
+        return (me + t) % devices
+
+    def copy(what, src, dst, peer):
+        return pltpu.make_async_remote_copy(
+            src_ref=src.at[peer],
+            dst_ref=dst.at[me],
+            send_sem=sems.at[2 * what, peer],
+            recv_sem=sems.at[2 * what + 1, me],
+            device_id=(peer // grp, peer % grp),
+            device_id_type=pl.DeviceIdType.MESH,
+        )
+
+    def wait_all(what, src, dst):
+        def one(t, carry):
+            peer = partner(t)
+            pltpu.make_async_remote_copy(
+                src_ref=src.at[peer],
+                dst_ref=dst.at[peer],
+                send_sem=sems.at[2 * what, peer],
+                recv_sem=sems.at[2 * what + 1, peer],
+                device_id=(peer // grp, peer % grp),
+                device_id_type=pl.DeviceIdType.MESH,
+            ).wait()
+            return carry
+
+        lax.fori_loop(1, devices, one, 0)
+
+    barrier = pltpu.get_barrier_semaphore()
+
+    def greet(t, carry):
+        peer = partner(t)
+        pl.semaphore_signal(
+            barrier,
+            inc=1,
+            device_id=(peer // grp, peer % grp),
+            device_id_type=pl.DeviceIdType.MESH,
+        )
+        return carry
+
+    lax.fori_loop(1, devices, greet, 0)
+    pl.semaphore_wait(barrier, devices - 1)
+
+    def ask(t, carry):
+        copy(0, req_ref, asked, partner(t)).start()
+        copy(1, req2_ref, asked2, partner(t)).start()
+        return carry
+
+    lax.fori_loop(1, devices, ask, 0)
+    asked[me] = req_ref[me]
+    asked2[me] = req2_ref[me]
+
+    step = 4 * LANES if rows.shape[0] % (4 * LANES) == 0 else LANES
+
+    def transpose(i, carry):
+        rows[tile(i, step), :] = table_ref[:, tile(i, step)].T.astype(jnp.float32)
+        return carry
+
+    lax.fori_loop(0, rows.shape[0] // step, transpose, 0)
+    wait_all(0, req_ref, asked)
+    wait_all(1, req2_ref, asked2)
+    to_scalars = pltpu.make_async_copy(asked, ids, local_sem)
+    to_scalars.start()
+    to_scalars.wait()
+
+    def pick(asker):
+        for j in range(cap):
+            block[j : j + 1, :] = rows[pl.ds(ids[asker, 0, j], 1), :]
+        return block[...].T.astype(jnp.bfloat16)
+
+    got[me] = pick(me)
+    send[partner(1)] = pick(partner(1))
+
+    def pick_and_send(t, carry):
+        send[partner(t)] = pick(partner(t))
+        copy(2, send, got, partner(t - 1)).start()
+        return carry
+
+    lax.fori_loop(2, devices, pick_and_send, 0)
+    onehot_slots(asked2, onehot)
+    copy(2, send, got, partner(devices - 1)).start()
+    count_slots(front_ref, own, near, cap)
+    wait_all(2, send, got)
+
+    lay_side_by_side(count1_ref, got, flat)
+    wide = 2 * LANES
+    fan_two, fan_one = float(front_ref.shape[0] - 1), float(seed_ref.shape[0] - 1)
+
+    def nodes_chunk(c, carry):
+        cols = tile(c, wide)
+        mine = dot32(flat[...], own[:, cols]).astype(jnp.bfloat16)
+        summed = (dot32(flat[...], near[:, cols]) / fan_two).astype(jnp.bfloat16)
+        preact = dot32(w1s_ref[...], mine) + dot32(w1n_ref[...], summed) + bias1_ref[...]
+        hidden = jnp.maximum(preact, 0.0).astype(jnp.bfloat16)
+        payload[:, cols] = dot32(w2_ref[...], hidden).astype(jnp.bfloat16)
+        return carry
+
+    lax.fori_loop(0, own.shape[1] // wide, nodes_chunk, 0)
+    cap_two = req2_ref.shape[2]
+
+    def chosen(asker):
+        return dot32(payload[...], onehot[:, tile(asker, cap_two)]).astype(jnp.bfloat16)
+
+    got2[me] = chosen(me)
+    send2[partner(1)] = chosen(partner(1))
+
+    def choose_and_send(t, carry):
+        send2[partner(t)] = chosen(partner(t))
+        copy(3, send2, got2, partner(t - 1)).start()
+        return carry
+
+    lax.fori_loop(2, devices, choose_and_send, 0)
+    bias2 = bias2_ref[...]
+    copy(3, send2, got2, partner(devices - 1)).start()
+    count_slots(seed_ref, seed_own, seed_near, cap_two)
+    wait_all(3, send2, got2)
+    lay_side_by_side(count2_ref, got2, flat2)
+    half = flat2.shape[0] // 2
+    self_term = dot32(flat2[:half], seed_own[...])
+    near_term = dot32(flat2[half:], seed_near[...]) / fan_one
+    out_ref[...] = (self_term + near_term)[: out_ref.shape[0]] + bias2
+
+
+def stacked_w2(w2_self, w2_neigh):
+    classes = w2_self.shape[0]
+    half = -(-classes // 16) * 16
+    pad = ((0, half - classes), (0, 0))
+    return jnp.concatenate([jnp.pad(w2_self, pad), jnp.pad(w2_neigh, pad)], axis=0)
 
 
 def mask_rows(received, counts, capacity):
@@ -16,7 +265,7 @@
     )
 
 
-def body(
+def take_body(
     table_t,
     req_rows,
     count1,
@@ -36,11 +285,11 @@
     table_rows = table_t.T
     picked_rows = jnp.take(
         table_rows,
-        lax.all_to_all(req_rows, ("shard", "grp"), split_axis=0, concat_axis=0, tiled=True),
+        lax.all_to_all(req_rows, AXES, split_axis=0, concat_axis=0, tiled=True),
         axis=0,
     )
     received = lax.all_to_all(
-        picked_rows, ("shard", "grp"), split_axis=0, concat_axis=0, tiled=True
+        picked_rows, AXES, split_axis=0, concat_axis=0, tiled=True
     )
     flat = mask_rows(received, count1, capacity)
     fanout_two = frontier_list.shape[0] - 1
@@ -57,10 +306,10 @@
     )
     chosen = jnp.take(
         payload,
-        lax.all_to_all(req2_rows, ("shard", "grp"), split_axis=0, concat_axis=0, tiled=True),
+        lax.all_to_all(req2_rows, AXES, split_axis=0, concat_axis=0, tiled=True),
         axis=0,
     )
-    got_back = lax.all_to_all(chosen, ("shard", "grp"), split_axis=0, concat_axis=0, tiled=True)
+    got_back = lax.all_to_all(chosen, AXES, split_axis=0, concat_axis=0, tiled=True)
     flat_two = mask_rows(got_back, count2, cap_two)
     fanout_one = seed_list.shape[0] - 1
     seed_nodes = seed_list.shape[1]
@@ -73,21 +322,106 @@
     return logits
 
 
+def body(
+    table_t,
+    req_rows,
+    count1,
+    frontier_list,
+    req2_rows,
+    count2,
+    seed_list,
+    w1_self,
+    w1_neigh,
+    bias1,
+    w2_self,
+    w2_neigh,
+    bias2,
+):
+    devices, cap = req_rows.shape
+    cap_two = req2_rows.shape[1]
+    nodes = frontier_list.shape[1]
+    if devices * max(cap, cap_two) * nodes > MATRIX_LIMIT:
+        return take_body(
+            table_t,
+            req_rows,
+            count1,
+            frontier_list,
+            req2_rows,
+            count2,
+            seed_list,
+            w1_self,
+            w1_neigh,
+            bias1,
+            w2_self,
+            w2_neigh,
+            bias2,
+        )
+    width, table_rows = table_t.shape
+    seeds = seed_list.shape[1]
+    w2 = stacked_w2(w2_self, w2_neigh)
+    slots, slots_two = devices * cap, devices * cap_two
+    bf16, f32, i32 = jnp.bfloat16, jnp.float32, jnp.int32
+    return pl.pallas_call(
+        functools.partial(whole_kernel, lax.axis_size(AXES[1])),
+        in_specs=[VMEM_ALL] * 3 + [SMEM_ALL] * 2 + [VMEM_ALL] * 7,
+        out_specs=VMEM_ALL,
+        out_shape=jax.ShapeDtypeStruct((w2_self.shape[0], seeds), f32),
+        scratch_shapes=[
+            pltpu.VMEM((devices, 1, cap), i32),
+            pltpu.VMEM((devices, 1, cap_two), i32),
+            pltpu.SMEM((devices, 1, cap), i32),
+            pltpu.VMEM((table_rows, width), f32),
+            pltpu.VMEM((cap, width), f32),
+            pltpu.VMEM((devices, width, cap), bf16),
+            pltpu.VMEM((devices, width, cap), bf16),
+            pltpu.VMEM((slots, nodes), bf16),
+            pltpu.VMEM((slots, nodes), bf16),
+            pltpu.VMEM((nodes, slots_two), bf16),
+            pltpu.VMEM((slots_two, seeds), bf16),
+            pltpu.VMEM((slots_two, seeds), bf16),
+            pltpu.VMEM((width, slots), bf16),
+            pltpu.VMEM((w2.shape[0], nodes), bf16),
+            pltpu.VMEM((devices, w2.shape[0], cap_two), bf16),
+            pltpu.VMEM((devices, w2.shape[0], cap_two), bf16),
+            pltpu.VMEM((w2.shape[0], slots_two), bf16),
+            pltpu.SemaphoreType.DMA,
+            pltpu.SemaphoreType.DMA((8, devices)),
+        ],
+        compiler_params=pltpu.CompilerParams(
+            vmem_limit_bytes=63 * MIB, collective_id=0, has_side_effects=True
+        ),
+    )(
+        table_t,
+        req_rows[:, None, :],
+        req2_rows[:, None, :],
+        count1,
+        count2,
+        frontier_list,
+        seed_list,
+        w1_self,
+        w1_neigh,
+        bias1[:, None],
+        w2,
+        bias2[:, None],
+    )
+
+
 def solution(mesh):
     in_specs = (
-        P(None, ("shard", "grp")),
-        P(("shard", "grp"), None),
-        P(("shard", "grp")),
-        P(None, ("shard", "grp")),
-        P(("shard", "grp"), None),
-        P(("shard", "grp")),
-        P(None, ("shard", "grp")),
-        P(),
-        P(),
-        P(),
-        P(),
-        P(),
-        P(),
-    )
-    out_specs = P(None, ("shard", "grp"))
-    return jax.shard_map(body, mesh=mesh, in_specs=in_specs, out_specs=out_specs, check_vma=False)
+        P(None, AXES),
+        P(AXES, None),
+        P(AXES),
+        P(None, AXES),
+        P(AXES, None),
+        P(AXES),
+        P(None, AXES),
+        P(),
+        P(),
+        P(),
+        P(),
+        P(),
+        P(),
+    )
+    return jax.shard_map(
+        body, mesh=mesh, in_specs=in_specs, out_specs=P(None, AXES), check_vma=False
+    )

time: 197 us -> 75.7 us (0.38)
  the two profiles are of different devices: /device:TPU:0 before, /device:TPU:15 now
where the time goes in v2:
time: 75.7 us; the launch traced here: 75.3 us
  Pallas kernels  66.6 us (88%)
  local copies, waits for them, and re-layouts  7.3 us (10%)
  other arithmetic  1.38 us (2%)
    pallas_call x1, Pallas kernels, body(): pl.pallas_call(functools.partial(whole_kernel, lax.axis_size(AXES[1])), i...  66.6 us
    unnamed x3, local copies, waits for them, and re-layouts  4.49 us

profile of v2, /device:TPU:15, one launch (start us, length us, event | category | flops | bytes accessed | tf_op | source)
XLA Modules:
  0.0 75.3 jit_solution(1743050145557256001)
XLA Ops:
  0.0 1.4 %copy.20.bias2_ref = f32[47,1]{1,0:T(8,128)} copy(f32[47,1]{0,1:T(1,128)} %bitcast.7) | data formatting | bytes 376 | tf_op jit(solution)/shard_map/broadcast_in_dim | solution.py:405
  1.4 1.4 %fusion.2.w2_ref = bf16[96,256]{1,0:T(8,128)(2,1)} fusion(bf16[47,256]{1,0:T(8,128)(2,1)} %param.24, bf16[47,256]{1,0:T(8,128)(2,1)} %param.23), kind=kLoop, calls=%fused_computation.4 | loop fusion | flops 196608 | bytes 97280 | tf_op jit(solution)/shard_map/concatenate | solution.py:253
  2.7 1.5 %copy.17.w1s_ref = bf16[256,100]{1,0:T(8,128)(2,1)} copy(bf16[256,100]{0,1:T(8,128)(2,1)} %param.20) | data formatting | bytes 102400 | tf_op args[7]
  4.3 1.5 %copy.18.w1n_ref = bf16[256,100]{1,0:T(8,128)(2,1)} copy(bf16[256,100]{0,1:T(8,128)(2,1)} %param.21) | data formatting | bytes 102400 | tf_op args[8]
  5.8 1.5 %copy.19.bias1_ref = f32[256,1]{1,0:T(8,128)} copy(f32[256,1]{0,1:T(1,128)} %bitcast.6) | data formatting | bytes 2048 | tf_op jit(solution)/shard_map/broadcast_in_dim | solution.py:403
  7.3 66.6 %shard_map.127 = f32[47,256]{1,0:T(8,128)} custom-call(bf16[100,19456]{1,0:T(8,128)(2,1)} %table_ref.1, s32[32,1,128]{2,1,0:T(1,128)} %bitcast.4, s32[32,1,128]{2,1,0:T(1,128)} %bitcast.5, s32[32]{0:T(128)} %count1_ref.1, s32[32]{0:T(128)} %count2_ref.1, s32[11,1024]{1,0:T(8,128)} %front_ref.1, s32[16,256]{1,0:T(8,128)} %seed_ref.1, ...), custom_call_target="tpu_custom_call" | custom-call | tf_op jit(solution)/shard_map/pallas_call | solution.py:364
  73.9 1.4 %copy.22 = f32[47,256]{1,0:T(8,128)} copy(f32[47,256]{1,0:T(8,128)} %shard_map.127) | data formatting | bytes 96256

commit v3 on v2

--- a/solution.py
+++ b/solution.py
@@ -36,7 +36,7 @@
     return pl.ds(pl.multiple_of(i * size, size), size)
 
 
-def count_slots(list_ref, own_ref, near_ref, cap):
+def count_slots(list_ref, own_ref, near_ref, cap, first, last):
     entries, nodes = list_ref.shape
     across = nodes // LANES
 
@@ -51,7 +51,7 @@
         near_ref[at, cols] = total
         return carry
 
-    lax.fori_loop(0, own_ref.shape[0] // cap * across, one, 0)
+    lax.fori_loop(first * across, last * across, one, 0)
 
 
 def onehot_slots(ids_ref, out_ref):
@@ -97,9 +97,13 @@
     w1s_ref,
     w1n_ref,
     bias1_ref,
-    w2_ref,
-    bias2_ref,
+    w2s_ref,
+    w2n_ref,
     out_ref,
+    table,
+    w1s,
+    w1n,
+    w2,
     asked,
     asked2,
     ids,
@@ -118,6 +122,7 @@
     got2,
     flat2,
     local_sem,
+    table_sem,
     sems,
 ):
     devices, _, cap = req_ref.shape
@@ -151,6 +156,8 @@
 
         lax.fori_loop(1, devices, one, 0)
 
+    load = pltpu.make_async_copy(table_ref, table, table_sem)
+    load.start()
     barrier = pltpu.get_barrier_semaphore()
 
     def greet(t, carry):
@@ -164,6 +171,8 @@
         return carry
 
     lax.fori_loop(1, devices, greet, 0)
+    early = devices // 8
+    count_slots(front_ref, own, near, cap, 0, early)
     pl.semaphore_wait(barrier, devices - 1)
 
     def ask(t, carry):
@@ -174,11 +183,19 @@
     lax.fori_loop(1, devices, ask, 0)
     asked[me] = req_ref[me]
     asked2[me] = req2_ref[me]
+    w1s[...] = w1s_ref[...].T
+    w1n[...] = w1n_ref[...].T
+    classes, half = w2s_ref.shape[0], w2.shape[0] // 2
+    w2[...] = jnp.zeros_like(w2)
+    w2[:classes] = w2s_ref[...]
+    w2[half : half + classes] = w2n_ref[...]
+    bias1 = jnp.broadcast_to(bias1_ref[...], (8, bias1_ref.shape[1])).T[:, :1]
+    load.wait()
 
     step = 4 * LANES if rows.shape[0] % (4 * LANES) == 0 else LANES
 
     def transpose(i, carry):
-        rows[tile(i, step), :] = table_ref[:, tile(i, step)].T.astype(jnp.float32)
+        rows[tile(i, step), :] = table[:, tile(i, step)].T.astype(jnp.float32)
         return carry
 
     lax.fori_loop(0, rows.shape[0] // step, transpose, 0)
@@ -204,7 +221,7 @@
     lax.fori_loop(2, devices, pick_and_send, 0)
     onehot_slots(asked2, onehot)
     copy(2, send, got, partner(devices - 1)).start()
-    count_slots(front_ref, own, near, cap)
+    count_slots(front_ref, own, near, cap, early, devices)
     wait_all(2, send, got)
 
     lay_side_by_side(count1_ref, got, flat)
@@ -215,9 +232,9 @@
         cols = tile(c, wide)
         mine = dot32(flat[...], own[:, cols]).astype(jnp.bfloat16)
         summed = (dot32(flat[...], near[:, cols]) / fan_two).astype(jnp.bfloat16)
-        preact = dot32(w1s_ref[...], mine) + dot32(w1n_ref[...], summed) + bias1_ref[...]
+        preact = dot32(w1s[...], mine) + dot32(w1n[...], summed) + bias1
         hidden = jnp.maximum(preact, 0.0).astype(jnp.bfloat16)
-        payload[:, cols] = dot32(w2_ref[...], hidden).astype(jnp.bfloat16)
+        payload[:, cols] = dot32(w2[...], hidden).astype(jnp.bfloat16)
         return carry
 
     lax.fori_loop(0, own.shape[1] // wide, nodes_chunk, 0)
@@ -235,22 +252,13 @@
         return carry
 
     lax.fori_loop(2, devices, choose_and_send, 0)
-    bias2 = bias2_ref[...]
     copy(3, send2, got2, partner(devices - 1)).start()
-    count_slots(seed_ref, seed_own, seed_near, cap_two)
+    count_slots(seed_ref, seed_own, seed_near, cap_two, 0, devices)
     wait_all(3, send2, got2)
     lay_side_by_side(count2_ref, got2, flat2)
-    half = flat2.shape[0] // 2
     self_term = dot32(flat2[:half], seed_own[...])
     near_term = dot32(flat2[half:], seed_near[...]) / fan_one
-    out_ref[...] = (self_term + near_term)[: out_ref.shape[0]] + bias2
-
-
-def stacked_w2(w2_self, w2_neigh):
-    classes = w2_self.shape[0]
-    half = -(-classes // 16) * 16
-    pad = ((0, half - classes), (0, 0))
-    return jnp.concatenate([jnp.pad(w2_self, pad), jnp.pad(w2_neigh, pad)], axis=0)
+    out_ref[...] = (self_term + near_term)[:classes]
 
 
 def mask_rows(received, counts, capacity):
@@ -358,15 +366,20 @@
         )
     width, table_rows = table_t.shape
     seeds = seed_list.shape[1]
-    w2 = stacked_w2(w2_self, w2_neigh)
+    hidden_width, classes = w1_self.shape[0], w2_self.shape[0]
+    rows_two = 2 * (-(-classes // 16) * 16)
     slots, slots_two = devices * cap, devices * cap_two
     bf16, f32, i32 = jnp.bfloat16, jnp.float32, jnp.int32
-    return pl.pallas_call(
+    logits = pl.pallas_call(
         functools.partial(whole_kernel, lax.axis_size(AXES[1])),
-        in_specs=[VMEM_ALL] * 3 + [SMEM_ALL] * 2 + [VMEM_ALL] * 7,
+        in_specs=[pl.BlockSpec(memory_space=pl.ANY)] + [VMEM_ALL] * 2 + [SMEM_ALL] * 2 + [VMEM_ALL] * 7,
         out_specs=VMEM_ALL,
-        out_shape=jax.ShapeDtypeStruct((w2_self.shape[0], seeds), f32),
+        out_shape=jax.ShapeDtypeStruct((classes, seeds), f32),
         scratch_shapes=[
+            pltpu.VMEM((width, table_rows), bf16),
+            pltpu.VMEM((hidden_width, width), bf16),
+            pltpu.VMEM((hidden_width, width), bf16),
+            pltpu.VMEM((rows_two, hidden_width), bf16),
             pltpu.VMEM((devices, 1, cap), i32),
             pltpu.VMEM((devices, 1, cap_two), i32),
             pltpu.SMEM((devices, 1, cap), i32),
@@ -380,10 +393,11 @@
             pltpu.VMEM((slots_two, seeds), bf16),
             pltpu.VMEM((slots_two, seeds), bf16),
             pltpu.VMEM((width, slots), bf16),
-            pltpu.VMEM((w2.shape[0], nodes), bf16),
-            pltpu.VMEM((devices, w2.shape[0], cap_two), bf16),
-            pltpu.VMEM((devices, w2.shape[0], cap_two), bf16),
-            pltpu.VMEM((w2.shape[0], slots_two), bf16),
+            pltpu.VMEM((rows_two, nodes), bf16),
+            pltpu.VMEM((devices, rows_two, cap_two), bf16),
+            pltpu.VMEM((devices, rows_two, cap_two), bf16),
+            pltpu.VMEM((rows_two, slots_two), bf16),
+            pltpu.SemaphoreType.DMA,
             pltpu.SemaphoreType.DMA,
             pltpu.SemaphoreType.DMA((8, devices)),
         ],
@@ -398,12 +412,13 @@
         count2,
         frontier_list,
         seed_list,
-        w1_self,
-        w1_neigh,
-        bias1[:, None],
-        w2,
-        bias2[:, None],
-    )
+        w1_self.T,
+        w1_neigh.T,
+        bias1[None, :],
+        w2_self,
+        w2_neigh,
+    )
+    return logits + bias2[:, None]
 
 
 def solution(mesh):

time: 75.7 us -> 65.6 us (0.87)
  local copies, waits for them, and re-layouts: 7.3 us -> 0.01 us
  Pallas kernels: 66.6 us -> 63.8 us
    unnamed x3 -> x2, local copies, waits for them, and re-layouts: 4.49 us -> 0.01 us
    broadcast_in_dim x2 -> x0, local copies, waits for them, and re-layouts: 2.81 us -> none  [the longest x1 1.45 us: body(): bias1[:, None]]
    pallas_call x1, Pallas kernels: 66.6 us -> 63.8 us  [body(): pl.pallas_call(functools.partial(whole_kernel, lax.axis_size(AXES[1])), i...]
    add x0 -> x1, other arithmetic: none -> 1.49 us  [body(): return logits + bias2[:, None]]
    concatenate x1 -> x0, other arithmetic: 1.38 us -> none  [stacked_w2(): jnp.concatenate([jnp.pad(w2_self, pad), jnp.pad(w2_neigh, pad)], axis=0)]
where the time goes in v3:
time: 65.6 us; the launch traced here: 65.4 us
  Pallas kernels  63.8 us (97%)
  other arithmetic  1.49 us (2%)
    pallas_call x1, Pallas kernels, body(): pl.pallas_call(functools.partial(whole_kernel, lax.axis_size(AXES[1])), i...  63.8 us
    add x1, other arithmetic, body(): return logits + bias2[:, None]  1.49 us

profile of v3, /device:TPU:15, one launch (start us, length us, event | category | flops | bytes accessed | tf_op | source)
XLA Modules:
  0.0 65.4 jit_solution(13002325038335293542)
XLA Ops:
  0.0 0.0 copy-start
  0.0 63.8 %shard_map.127 = f32[47,256]{1,0:T(8,128)} custom-call(bf16[100,19456]{1,0:T(8,128)(2,1)} %table_ref.1, s32[32,1,128]{2,1,0:T(1,128)} %bitcast.7, s32[32,1,128]{2,1,0:T(1,128)} %bitcast.8, s32[32]{0:T(128)} %count1_ref.1, s32[32]{0:T(128)} %count2_ref.1, s32[11,1024]{1,0:T(8,128)} %front_ref.1, s32[16,256]{1,0:T(8,128)} %seed_ref.1, ...), custom_call_target="tpu_custom_call" | custom-call | tf_op jit(solution)/shard_map/pallas_call | solution.py:373
  63.8 0.0 copy-done
  63.9 1.5 %broadcast_add_fusion = f32[47,256]{1,0:T(8,128)} fusion(f32[47,256]{1,0:T(8,128)} %shard_map.127, f32[47]{0:T(128)S(1)} %copy-done), kind=kLoop, calls=%fused_computation | loop fusion | flops 12032 | bytes 96444 | tf_op jit(solution)/shard_map/add | solution.py:421
Async XLA Ops:
  0.0 63.8 %copy-start = (f32[47]{0:T(128)S(1)}, f32[47]{0:T(128)}, u32[]{:S(2)}) copy-start(f32[47]{0:T(128)} %param.25) | copy-start | bytes 568

commit v4 on v3

--- a/solution.py
+++ b/solution.py
@@ -26,47 +26,39 @@
     return jnp.where(inside, local, -1).astype(jnp.float32)
 
 
-def hits(row, span):
-    ids = lax.broadcasted_iota(jnp.int32, (span, row.shape[1]), 0)
-    ids = ids.astype(jnp.float32).astype(jnp.bfloat16)
-    return jnp.where(tall(row, span) == ids, jnp.ones((), jnp.bfloat16), jnp.zeros((), jnp.bfloat16))
+def places(span):
+    ids = lax.broadcasted_iota(jnp.int32, (span, LANES), 0)
+    return ids.astype(jnp.float32).astype(jnp.bfloat16)
+
+
+def hits(row, ids):
+    one, zero = jnp.ones((), jnp.bfloat16), jnp.zeros((), jnp.bfloat16)
+    return jnp.where(tall(row, ids.shape[0]) == ids, one, zero)
 
 
 def tile(i, size=LANES):
     return pl.ds(pl.multiple_of(i * size, size), size)
 
 
-def count_slots(list_ref, own_ref, near_ref, cap, first, last):
-    entries, nodes = list_ref.shape
-    across = nodes // LANES
+def count_tile(list_ref, own_ref, near_ref, ids, owner, c):
+    cap = ids.shape[0]
+    cols, at = tile(c), tile(owner, cap)
+    local = local_rows(list_ref[:, cols], owner * cap, cap)
+    own_ref[at, cols] = hits(local[0:1], ids)
+    total = hits(local[1:2], ids)
+    for k in range(2, list_ref.shape[0]):
+        total = total + hits(local[k : k + 1], ids)
+    near_ref[at, cols] = total
+
+
+def count_slots(list_ref, own_ref, near_ref, ids, first, last):
+    across = list_ref.shape[1] // LANES
 
     def one(i, carry):
-        owner, cols = i // across, tile(i % across)
-        at = tile(owner, cap)
-        local = local_rows(list_ref[:, cols], owner * cap, cap)
-        own_ref[at, cols] = hits(local[0:1], cap)
-        total = hits(local[1:2], cap)
-        for k in range(2, entries):
-            total = total + hits(local[k : k + 1], cap)
-        near_ref[at, cols] = total
+        count_tile(list_ref, own_ref, near_ref, ids, i // across, i % across)
         return carry
 
     lax.fori_loop(first * across, last * across, one, 0)
-
-
-def onehot_slots(ids_ref, out_ref):
-    nodes = out_ref.shape[0]
-    devices, _, cap = ids_ref.shape
-
-    def one(asker, carry):
-        wanted = ids_ref[asker]
-        for b in range(nodes // LANES):
-            out_ref[b * LANES : (b + 1) * LANES, tile(asker, cap)] = hits(
-                local_rows(wanted, b * LANES, LANES), LANES
-            )
-        return carry
-
-    lax.fori_loop(0, devices, one, 0)
 
 
 def lay_side_by_side(counts_ref, blocks_ref, flat):
@@ -113,7 +105,6 @@
     got,
     own,
     near,
-    onehot,
     seed_own,
     seed_near,
     flat,
@@ -126,6 +117,7 @@
     sems,
 ):
     devices, _, cap = req_ref.shape
+    cap_two = req2_ref.shape[2]
     me = lax.axis_index(AXES[0]) * grp + lax.axis_index(AXES[1])
 
     def partner(t):
@@ -171,8 +163,9 @@
         return carry
 
     lax.fori_loop(1, devices, greet, 0)
-    early = devices // 8
-    count_slots(front_ref, own, near, cap, 0, early)
+    marks, marks2, node_marks = places(cap), places(cap_two), places(LANES)
+    early = 2
+    count_slots(front_ref, own, near, marks, 0, early)
     pl.semaphore_wait(barrier, devices - 1)
 
     def ask(t, carry):
@@ -205,23 +198,28 @@
     to_scalars.start()
     to_scalars.wait()
 
-    def pick(asker):
-        for j in range(cap):
-            block[j : j + 1, :] = rows[pl.ds(ids[asker, 0, j], 1), :]
+    across = front_ref.shape[1] // LANES
+    share = -(-cap // across)
+
+    def pick(asker, owner=None):
+        for c in range(across):
+            for j in range(c * share, min(cap, (c + 1) * share)):
+                block[j : j + 1, :] = rows[pl.ds(ids[asker, 0, j], 1), :]
+            if owner is not None:
+                count_tile(front_ref, own, near, marks, owner, c)
         return block[...].T.astype(jnp.bfloat16)
 
     got[me] = pick(me)
     send[partner(1)] = pick(partner(1))
 
     def pick_and_send(t, carry):
-        send[partner(t)] = pick(partner(t))
+        send[partner(t)] = pick(partner(t), t)
         copy(2, send, got, partner(t - 1)).start()
         return carry
 
-    lax.fori_loop(2, devices, pick_and_send, 0)
-    onehot_slots(asked2, onehot)
+    lax.fori_loop(early, devices, pick_and_send, 0)
+    count_slots(seed_ref, seed_own, seed_near, marks2, 0, 1)
     copy(2, send, got, partner(devices - 1)).start()
-    count_slots(front_ref, own, near, cap, early, devices)
     wait_all(2, send, got)
 
     lay_side_by_side(count1_ref, got, flat)
@@ -238,10 +236,14 @@
         return carry
 
     lax.fori_loop(0, own.shape[1] // wide, nodes_chunk, 0)
-    cap_two = req2_ref.shape[2]
 
     def chosen(asker):
-        return dot32(payload[...], onehot[:, tile(asker, cap_two)]).astype(jnp.bfloat16)
+        wanted = asked2[asker]
+        select = [
+            hits(local_rows(wanted, b * LANES, LANES), node_marks)
+            for b in range(payload.shape[1] // LANES)
+        ]
+        return dot32(payload[...], jnp.concatenate(select, axis=0)).astype(jnp.bfloat16)
 
     got2[me] = chosen(me)
     send2[partner(1)] = chosen(partner(1))
@@ -252,8 +254,9 @@
         return carry
 
     lax.fori_loop(2, devices, choose_and_send, 0)
+    count_slots(seed_ref, seed_own, seed_near, marks2, 1, 2)
     copy(3, send2, got2, partner(devices - 1)).start()
-    count_slots(seed_ref, seed_own, seed_near, cap_two, 0, devices)
+    count_slots(seed_ref, seed_own, seed_near, marks2, 2, devices)
     wait_all(3, send2, got2)
     lay_side_by_side(count2_ref, got2, flat2)
     self_term = dot32(flat2[:half], seed_own[...])
@@ -389,7 +392,6 @@
             pltpu.VMEM((devices, width, cap), bf16),
             pltpu.VMEM((slots, nodes), bf16),
             pltpu.VMEM((slots, nodes), bf16),
-            pltpu.VMEM((nodes, slots_two), bf16),
             pltpu.VMEM((slots_two, seeds), bf16),
             pltpu.VMEM((slots_two, seeds), bf16),
             pltpu.VMEM((width, slots), bf16),

time: 65.6 us -> 65.6 us (level)
  no operation moved by 1% of the time
where the time goes in v4:
time: 65.6 us; the launch traced here: 65.4 us
  Pallas kernels  63.8 us (97%)
  other arithmetic  1.49 us (2%)
    pallas_call x1, Pallas kernels, body(): pl.pallas_call(functools.partial(whole_kernel, lax.axis_size(AXES[1])), i...  63.8 us
    add x1, other arithmetic, body(): return logits + bias2[:, None]  1.49 us

profile of v4, /device:TPU:15, one launch (start us, length us, event | category | flops | bytes accessed | tf_op | source)
XLA Modules:
  0.0 65.4 jit_solution(11783103809669574072)
XLA Ops:
  0.0 0.0 copy-start
  0.0 63.8 %shard_map.127 = f32[47,256]{1,0:T(8,128)} custom-call(bf16[100,19456]{1,0:T(8,128)(2,1)} %table_ref.1, s32[32,1,128]{2,1,0:T(1,128)} %bitcast.7, s32[32,1,128]{2,1,0:T(1,128)} %bitcast.8, s32[32]{0:T(128)} %count1_ref.1, s32[32]{0:T(128)} %count2_ref.1, s32[11,1024]{1,0:T(8,128)} %front_ref.1, s32[16,256]{1,0:T(8,128)} %seed_ref.1, ...), custom_call_target="tpu_custom_call" | custom-call | tf_op jit(solution)/shard_map/pallas_call | solution.py:376
  63.8 0.0 copy-done
  63.9 1.5 %broadcast_add_fusion = f32[47,256]{1,0:T(8,128)} fusion(f32[47,256]{1,0:T(8,128)} %shard_map.127, f32[47]{0:T(128)S(1)} %copy-done), kind=kLoop, calls=%fused_computation | loop fusion | flops 12032 | bytes 96444 | tf_op jit(solution)/shard_map/add | solution.py:423
Async XLA Ops:
  0.0 63.8 %copy-start = (f32[47]{0:T(128)S(1)}, f32[47]{0:T(128)}, u32[]{:S(2)}) copy-start(f32[47]{0:T(128)} %param.25) | copy-start | bytes 568

commit v5 on v4

--- a/solution.py
+++ b/solution.py
@@ -40,9 +40,9 @@
     return pl.ds(pl.multiple_of(i * size, size), size)
 
 
-def count_tile(list_ref, own_ref, near_ref, ids, owner, c):
+def count_tile(list_ref, own_ref, near_ref, ids, owner, c, place):
     cap = ids.shape[0]
-    cols, at = tile(c), tile(owner, cap)
+    cols, at = tile(c), tile(place, cap)
     local = local_rows(list_ref[:, cols], owner * cap, cap)
     own_ref[at, cols] = hits(local[0:1], ids)
     total = hits(local[1:2], ids)
@@ -51,26 +51,28 @@
     near_ref[at, cols] = total
 
 
-def count_slots(list_ref, own_ref, near_ref, ids, first, last):
+def count_slots(list_ref, own_ref, near_ref, ids, first, last, owner_of=lambda place: place):
     across = list_ref.shape[1] // LANES
 
     def one(i, carry):
-        count_tile(list_ref, own_ref, near_ref, ids, i // across, i % across)
+        place = i // across
+        count_tile(list_ref, own_ref, near_ref, ids, owner_of(place), i % across, place)
         return carry
 
     lax.fori_loop(first * across, last * across, one, 0)
 
 
-def lay_side_by_side(counts_ref, blocks_ref, flat):
-    devices, width, cap = blocks_ref.shape
+def lay_side_by_side(counts_ref, blocks_ref, flat, first, last, owner_of=lambda place: place):
+    _, width, cap = blocks_ref.shape
     slot = lax.broadcasted_iota(jnp.int32, (width, cap), 1)
 
-    def one(o, carry):
+    def one(place, carry):
+        o = owner_of(place)
         live = jnp.where(slot < counts_ref[o], blocks_ref[o].astype(jnp.float32), 0.0)
-        flat[:, tile(o, cap)] = live.astype(jnp.bfloat16)
-        return carry
-
-    lax.fori_loop(0, devices, one, 0)
+        flat[:, tile(place, cap)] = live.astype(jnp.bfloat16)
+        return carry
+
+    lax.fori_loop(first, last, one, 0)
 
 
 def dot32(a, b):
@@ -108,6 +110,7 @@
     seed_own,
     seed_near,
     flat,
+    sums,
     payload,
     send2,
     got2,
@@ -133,7 +136,7 @@
             device_id_type=pl.DeviceIdType.MESH,
         )
 
-    def wait_all(what, src, dst):
+    def wait_all(what, src, dst, first=1, last=devices):
         def one(t, carry):
             peer = partner(t)
             pltpu.make_async_remote_copy(
@@ -146,7 +149,7 @@
             ).wait()
             return carry
 
-        lax.fori_loop(1, devices, one, 0)
+        lax.fori_loop(first, last, one, 0)
 
     load = pltpu.make_async_copy(table_ref, table, table_sem)
     load.start()
@@ -165,7 +168,7 @@
     lax.fori_loop(1, devices, greet, 0)
     marks, marks2, node_marks = places(cap), places(cap_two), places(LANES)
     early = 2
-    count_slots(front_ref, own, near, marks, 0, early)
+    count_slots(front_ref, own, near, marks, 0, early, partner)
     pl.semaphore_wait(barrier, devices - 1)
 
     def ask(t, carry):
@@ -201,12 +204,12 @@
     across = front_ref.shape[1] // LANES
     share = -(-cap // across)
 
-    def pick(asker, owner=None):
+    def pick(asker, place=None):
         for c in range(across):
             for j in range(c * share, min(cap, (c + 1) * share)):
                 block[j : j + 1, :] = rows[pl.ds(ids[asker, 0, j], 1), :]
-            if owner is not None:
-                count_tile(front_ref, own, near, marks, owner, c)
+            if place is not None:
+                count_tile(front_ref, own, near, marks, partner(place), c, place)
         return block[...].T.astype(jnp.bfloat16)
 
     got[me] = pick(me)
@@ -220,16 +223,30 @@
     lax.fori_loop(early, devices, pick_and_send, 0)
     count_slots(seed_ref, seed_own, seed_near, marks2, 0, 1)
     copy(2, send, got, partner(devices - 1)).start()
-    wait_all(2, send, got)
-
-    lay_side_by_side(count1_ref, got, flat)
     wide = 2 * LANES
+    groups = 4 if devices % 4 == 0 else 1
+    many = devices // groups
+    for g in reversed(range(groups)):
+        wait_all(2, send, got, max(1, g * many), (g + 1) * many)
+        lay_side_by_side(count1_ref, got, flat, g * many, (g + 1) * many, partner)
+        depth = slice(g * many * cap, (g + 1) * many * cap)
+
+        def add_group(c, carry, g=g, depth=depth):
+            cols = tile(c, wide)
+            for which, matrix in enumerate((own, near)):
+                part = dot32(flat[:, depth], matrix[depth, cols])
+                sums[which, :, cols] = part if g == groups - 1 else sums[which, :, cols] + part
+            return carry
+
+        if g > 0:
+            lax.fori_loop(0, own.shape[1] // wide, add_group, 0)
     fan_two, fan_one = float(front_ref.shape[0] - 1), float(seed_ref.shape[0] - 1)
 
     def nodes_chunk(c, carry):
         cols = tile(c, wide)
-        mine = dot32(flat[...], own[:, cols]).astype(jnp.bfloat16)
-        summed = (dot32(flat[...], near[:, cols]) / fan_two).astype(jnp.bfloat16)
+        add_group(c, 0)
+        mine = sums[0, :, cols].astype(jnp.bfloat16)
+        summed = (sums[1, :, cols] / fan_two).astype(jnp.bfloat16)
         preact = dot32(w1s[...], mine) + dot32(w1n[...], summed) + bias1
         hidden = jnp.maximum(preact, 0.0).astype(jnp.bfloat16)
         payload[:, cols] = dot32(w2[...], hidden).astype(jnp.bfloat16)
@@ -258,7 +275,7 @@
     copy(3, send2, got2, partner(devices - 1)).start()
     count_slots(seed_ref, seed_own, seed_near, marks2, 2, devices)
     wait_all(3, send2, got2)
-    lay_side_by_side(count2_ref, got2, flat2)
+    lay_side_by_side(count2_ref, got2, flat2, 0, devices)
     self_term = dot32(flat2[:half], seed_own[...])
     near_term = dot32(flat2[half:], seed_near[...]) / fan_one
     out_ref[...] = (self_term + near_term)[:classes]
@@ -395,6 +412,7 @@
             pltpu.VMEM((slots_two, seeds), bf16),
             pltpu.VMEM((slots_two, seeds), bf16),
             pltpu.VMEM((width, slots), bf16),
+            pltpu.VMEM((2, width, nodes), f32),
             pltpu.VMEM((rows_two, nodes), bf16),
             pltpu.VMEM((devices, rows_two, cap_two), bf16),
             pltpu.VMEM((devices, rows_two, cap_two), bf16),

time: 65.6 us -> 65.9 us (level)
  no operation moved by 1% of the time
where the time goes in v5:
time: 65.9 us; the launch traced here: 65.7 us
  Pallas kernels  64.2 us (97%)
  other arithmetic  1.49 us (2%)
    pallas_call x1, Pallas kernels, body(): pl.pallas_call(functools.partial(whole_kernel, lax.axis_size(AXES[1])), i...  64.2 us
    add x1, other arithmetic, body(): return logits + bias2[:, None]  1.49 us

profile of v5, /device:TPU:15, one launch (start us, length us, event | category | flops | bytes accessed | tf_op | source)
XLA Modules:
  0.0 65.7 jit_solution(1843915496464106531)
XLA Ops:
  0.0 0.0 copy-start
  0.0 64.2 %shard_map.127 = f32[47,256]{1,0:T(8,128)} custom-call(bf16[100,19456]{1,0:T(8,128)(2,1)} %table_ref.1, s32[32,1,128]{2,1,0:T(1,128)} %bitcast.7, s32[32,1,128]{2,1,0:T(1,128)} %bitcast.8, s32[32]{0:T(128)} %count1_ref.1, s32[32]{0:T(128)} %count2_ref.1, s32[11,1024]{1,0:T(8,128)} %front_ref.1, s32[16,256]{1,0:T(8,128)} %seed_ref.1, ...), custom_call_target="tpu_custom_call" | custom-call | tf_op jit(solution)/shard_map/pallas_call | solution.py:393
  64.2 0.0 copy-done
  64.2 1.5 %broadcast_add_fusion = f32[47,256]{1,0:T(8,128)} fusion(f32[47,256]{1,0:T(8,128)} %shard_map.127, f32[47]{0:T(128)S(1)} %copy-done), kind=kLoop, calls=%fused_computation | loop fusion | flops 12032 | bytes 96444 | tf_op jit(solution)/shard_map/add | solution.py:441
Async XLA Ops:
  0.0 64.2 %copy-start = (f32[47]{0:T(128)S(1)}, f32[47]{0:T(128)}, u32[]{:S(2)}) copy-start(f32[47]{0:T(128)} %param.25) | copy-start | bytes 568
